TPU v7x, 32 devices: a whole 2x2x4 slice. The times are simulated.
32 devices in a mesh: tensor: 4 (over y, core), expert: 4 (over z), dp: 2 (over x).
Axes of the slice: x: 2, y: 2, z: 4, core: 2. Of those that a mesh axis runs over, the one named last changes fastest.
Arguments:
- grad_out: bfloat16 [512, 4096], P(('expert', 'dp')), may hold values from -6 to 6
- route_ids: int32 [512, 8], P(('expert', 'dp')), may hold values from 0 to 127, all different within a row; in each aligned block of 64 rows (0 to 63, 64 to 127, ...) at most 6 rows name the same one
- route_probs: bfloat16 [512, 8], P(('expert', 'dp')), may hold values from 0.019897461 to 0.5
- gate_act: bfloat16 [2, 128, 24, 768], P('dp', 'expert', None, 'tensor'), may hold values from -8 to 8
- up_act: bfloat16 [2, 128, 24, 768], P('dp', 'expert', None, 'tensor'), may hold values from -6 to 6
- w_down: bfloat16 [128, 768, 4096], P('expert', 'tensor'), may hold values from -0.21875 to 0.21875
Outputs:
- grad_gate: bfloat16 [2, 128, 24, 768], P('dp', 'expert', None, 'tensor')
- grad_up: bfloat16 [2, 128, 24, 768], P('dp', 'expert', None, 'tensor')
- grad_w_down: bfloat16 [128, 768, 4096], P('expert', 'tensor', 'dp')
- grad_probs: float32 [512, 8], P(('expert', 'dp'))
Inputs may be any that keep to these rules, and one draw needn't show every extreme that they name: `route_ids`: each row names 8 different experts. Within the 64 rows of one index pair of expert and dp no expert is named more than 6 times, and in every draw some expert is named exactly 6 times there.
All inputs are finite; a program needn't handle non-finite values.
Results may differ from a plain program's by a relative error of at most 0.009.
Values may be sent and summed in bfloat16 or wider, within the bound.
A program may use at most 192 MiB of HBM per device.

v0:
```python
import jax
import jax.numpy as jnp
from jax import lax
from jax.sharding import PartitionSpec as P


def on_device(grad_out, route_ids, route_probs, gate_act, up_act, w_down):
    tok_count = grad_out.shape[0]
    top_count = route_ids.shape[1]
    expert_count = lax.axis_size("expert")
    tensor_count = lax.axis_size("tensor")
    local_experts = w_down.shape[0]
    experts = local_experts * expert_count
    slot_count = gate_act.shape[2]
    capacity = slot_count // expert_count
    model_width = grad_out.shape[1]
    quarter = model_width // tensor_count
    route_flat = route_ids.reshape(-1)
    expert_iota = lax.broadcasted_iota(jnp.int32, (1, experts), 1)
    matches = (route_flat[:, None] == expert_iota).astype(jnp.int32)
    earlier = jnp.cumsum(matches, axis=0) - matches
    position = jnp.sum(earlier * matches, axis=1)
    target = route_flat * capacity + position
    cell_iota = lax.broadcasted_iota(jnp.int32, (1, experts * capacity), 1)
    chosen = target[:, None] == cell_iota
    chosen_weight = chosen.astype(jnp.float32)
    token_chosen = jnp.sum(
        chosen_weight.reshape(tok_count, top_count, experts * capacity), axis=1
    ).astype(jnp.bfloat16)
    own_columns = lax.dynamic_slice_in_dim(grad_out, lax.axis_index("tensor") * quarter, quarter, 1)
    send_rows = jnp.einsum(
        "nf,nd->fd", token_chosen, own_columns, preferred_element_type=jnp.float32
    ).astype(jnp.bfloat16)
    send_probs = jnp.sum(
        chosen_weight * route_probs.reshape(-1).astype(jnp.float32)[:, None], axis=0
    ).astype(jnp.bfloat16)
    send_rows = send_rows.reshape(expert_count, local_experts, capacity, quarter)
    send_probs = send_probs.reshape(expert_count, local_experts, capacity)
    arrived_rows, arrived_probs = (
        lax.all_to_all(send_rows, "expert", split_axis=0, concat_axis=0, tiled=True),
        lax.all_to_all(send_probs, "expert", split_axis=0, concat_axis=0, tiled=True),
    )
    gathered = lax.all_gather(arrived_rows, "tensor", axis=3, tiled=True)
    slot_rows = jnp.transpose(gathered, (1, 0, 2, 3)).reshape(
        local_experts, slot_count, model_width
    )
    slot_probs = (
        jnp.transpose(arrived_probs, (1, 0, 2))
        .reshape(local_experts, slot_count)
        .astype(jnp.float32)
    )
    gate_pre = gate_act[0].astype(jnp.float32)
    up_pre = up_act[0].astype(jnp.float32)
    grad_hidden = jnp.einsum("jsd,jfd->jsf", slot_rows, w_down, preferred_element_type=jnp.float32)
    sigmoid_gate = jax.nn.sigmoid(gate_pre)
    silu_gate = gate_pre * sigmoid_gate
    hidden = (silu_gate * up_pre).astype(jnp.bfloat16)
    partial_dot = jnp.sum(grad_hidden * hidden.astype(jnp.float32), axis=2)
    grad_scaled = slot_probs[:, :, None] * grad_hidden
    grad_up = (grad_scaled * silu_gate).astype(jnp.bfloat16)
    grad_gate = (
        grad_scaled * up_pre * sigmoid_gate * (1.0 + gate_pre * (1.0 - sigmoid_gate))
    ).astype(jnp.bfloat16)
    scaled_rows = (slot_probs[:, :, None] * slot_rows.astype(jnp.float32)).astype(jnp.bfloat16)
    replica_count = lax.axis_size("dp")
    column_count = model_width // replica_count
    split_rows = jnp.transpose(
        scaled_rows.reshape(local_experts, slot_count, replica_count, column_count), (2, 0, 1, 3)
    )
    columns = lax.all_to_all(split_rows, "dp", split_axis=0, concat_axis=0, tiled=True)
    initial = jnp.zeros((local_experts, hidden.shape[2], column_count), jnp.float32)
    hidden_block = lax.all_gather(hidden[None], "dp", axis=0, tiled=True)

    def add_member(member, summed):
        hid_one = lax.dynamic_index_in_dim(hidden_block, member, 0, keepdims=False)
        col_one = lax.dynamic_index_in_dim(columns, member, 0, keepdims=False)
        term = jnp.einsum("jsf,jsd->jfd", hid_one, col_one, preferred_element_type=jnp.float32)
        rounded = lax.optimization_barrier(term.astype(jnp.bfloat16))
        return summed + rounded.astype(jnp.float32)

    grad_weight = lax.fori_loop(0, hidden_block.shape[0], add_member, initial).astype(jnp.bfloat16)
    prob_cells = jnp.transpose(
        partial_dot.reshape(local_experts, expert_count, capacity), (1, 0, 2)
    )
    prob_cells = lax.psum(prob_cells, "tensor")
    returned = lax.all_to_all(prob_cells, "expert", split_axis=0, concat_axis=0, tiled=True)
    returned_flat = returned.reshape(-1)
    grad_probs = jnp.sum(jnp.where(chosen, returned_flat[None, :], 0.0), axis=1).reshape(
        tok_count, top_count
    )
    return (grad_gate[None], grad_up[None], grad_weight, grad_probs)


def solution(mesh):
    placed = (
        P(("expert", "dp"), None),
        P(("expert", "dp"), None),
        P(("expert", "dp"), None),
        P("dp", "expert", None, "tensor"),
        P("dp", "expert", None, "tensor"),
        P("expert", "tensor", None),
    )
    return jax.shard_map(
        on_device,
        mesh=mesh,
        in_specs=placed,
        out_specs=(
            P("dp", "expert", None, "tensor"),
            P("dp", "expert", None, "tensor"),
            P("expert", "tensor", "dp"),
            P(("expert", "dp"), None),
        ),
        check_vma=False,
    )
```

profile of v0, /device:TPU:0, one launch (start us, length us, event | category | flops | bytes accessed | tf_op | source)
XLA Modules:
  0.0 410.9 jit_solution(18393939632050930372)
XLA Ops:
  7.2 0.8 copy.59
  9.1 0.7 multiply_add_fusion
  9.8 0.5 convert_reduce_fusion
  10.4 1.7 convolution_convert_fusion.1
  12.1 2.6 reshape.88
  14.7 0.9 copy.68
  15.6 43.2 %all_to_all.20 = bf16[4,32,6,1024]{3,1,2,0:T(8,128)(2,1)} all-to-all(bf16[4,32,6,1024]{3,1,2,0:T(8,128)(2,1)S(1)} %copy.68), channel_id=1, replica_groups=mesh['tensor'=4,'expert'=4,'dp'=2] {'expert'}, dimensions={0} | all-to-all | bytes 3145728 | tf_op jit(solution)/shard_map/all_to_all | solution.py:40
  58.8 45.7 %all-gather.2.cloned.1.call-done = bf16[4,32,6,4096]{3,1,2,0:T(8,128)(2,1)} async-done(((bf16[4,32,6,1024]{3,1,2,0:T(8,128)(2,1)}), bf16[4,32,6,4096]{3,1,2,0:T(8,128)(2,1)}) %all-gather.2.cloned.1.call-update) | async-done | bytes 6291472 | tf_op jit(solution)/shard_map/all_gather | solution.py:43
  104.5 21.3 %multiply_reduce_fusion = (f32[32,24]{1,0:T(8,128)S(1)}, f32[32,24,192]{2,1,0:T(8,128)S(1)}) fusion(bf16[1,32,24,192]{3,2,1,0:T(8,128)(2,1)S(1)} %copy-done.2, bf16[1,32,24,192]{3,2,1,0:T(8,128)(2,1)S(1)} %copy-done.3, bf16[32,192,4096]{2,1,0:T(8,128)(2,1)} %param.13, bf16[32,24,4096]{2,0,1:T(8,128)(2,1)} %bitcast.94), kind=kOutput, calls=%fused_computation.40 | convolution fusion | flops 1209580800 | bytes 57805824 | tf_op jit(solution)/shard_map/jsd,jfd->jsf/dot_general | solution.py:54
  125.9 10.2 %psum.7 = f32[4,32,6]{1,2,0:T(8,128)S(1)} all-reduce(f32[4,32,6]{1,2,0:T(8,128)S(1)} %bitcast.98), channel_id=1, replica_groups=mesh['tensor'=4,'expert'=4,'dp'=2] {'tensor'}, use_global_device_ids=true, to_apply=%region_8.9 | all-reduce | flops 768 | bytes 6144 | tf_op jit(solution)/shard_map/psum | solution.py:85
  136.1 0.7 reshape.97
  136.8 4.8 %all-to-all-start.3 = ((f32[4,1,192]{2,1,0:T(1,128)}), f32[4,1,192]{2,1,0:T(1,128)S(1)}, u32[]{:S(2)}, u32[]{:S(2)}) async-start(f32[4,1,192]{2,1,0:T(1,128)} %reshape.97), calls=%async_computation.3 | async-start | bytes 8192 | tf_op jit(solution)/shard_map/all_to_all | solution.py:86
  141.7 5.4 %all-to-all-done.3 = f32[4,1,192]{2,1,0:T(1,128)S(1)} async-done(((f32[4,1,192]{2,1,0:T(1,128)}), f32[4,1,192]{2,1,0:T(1,128)S(1)}, u32[]{:S(2)}, u32[]{:S(2)}) %all-to-all-start.3) | async-done | bytes 3104 | tf_op jit(solution)/shard_map/all_to_all | solution.py:86
  147.6 0.7 reduce
  149.3 0.7 copy.64
  150.0 3.4 all-to-all-start
  153.4 9.3 %bitcast_convert_fusion = f32[32,4,6,4096]{3,0,2,1:T(8,128)} fusion(bf16[4,32,6,4096]{3,1,2,0:T(8,128)(2,1)} %all-gather.2.cloned.1.call-done), kind=kLoop, calls=%fused_computation.9 | loop fusion | flops 3145728 | bytes 18874368 | tf_op jit(solution)/shard_map/convert_element_type | solution.py:64
  162.7 16.9 %reshape.96 = f32[32,24,2,2048]{3,2,0,1:T(2,128)} reshape(f32[32,4,6,4096]{3,0,2,1:T(8,128)} %bitcast_convert_fusion) | data formatting | bytes 25165824 | tf_op jit(solution)/shard_map/convert_element_type | solution.py:64
  179.6 8.0 %fusion.3 = bf16[2,32,24,2048]{3,0,1,2:T(2,128)(2,1)S(1)} fusion(f32[32,24,2,2048]{3,2,0,1:T(2,128)} %reshape.96, f32[32,24]{0,1:T(8,128)S(1)} %reshape.93), kind=kLoop, calls=%fused_computation.8 | loop fusion | flops 6291456 | bytes 18877440 | tf_op jit(solution)/shard_map/transpose | solution.py:67
  187.6 5.6 %copy.70 = bf16[2,32,24,2048]{3,1,2,0:T(8,128)(2,1)} copy(bf16[2,32,24,2048]{3,0,1,2:T(2,128)(2,1)S(1)} %fusion.3) | data formatting | bytes 12582912 | tf_op jit(solution)/shard_map/transpose | solution.py:67
  193.2 6.2 %all-to-all-start.2 = ((bf16[2,32,24,2048]{3,1,2,0:T(8,128)(2,1)}), bf16[2,32,24,2048]{3,1,2,0:T(8,128)(2,1)}, u32[]{:S(2)}, u32[]{:S(2)}) async-start(bf16[2,32,24,2048]{3,1,2,0:T(8,128)(2,1)} %copy.70), calls=%async_computation.2 | async-start | bytes 12582912 | tf_op jit(solution)/shard_map/all_to_all | solution.py:70
  199.8 76.2 %all_gather.7 = bf16[2,32,24,192]{3,2,1,0:T(8,128)(2,1)S(1)} all-gather(bf16[1,32,24,192]{3,2,1,0:T(8,128)(2,1)S(1)} %fusion.15), channel_id=1, replica_groups=mesh['tensor'=4,'expert'=4,'dp'=2] {'dp'}, dimensions={0}, use_global_device_ids=true | all-gather | bytes 884736 | tf_op jit(solution)/shard_map/all_gather | solution.py:72
  276.1 0.7 copy.74
  276.8 1.3 fusion.23
  278.2 99.9 %while.14 = (s32[]{:T(128)}, f32[32,192,2048]{2,1,0:T(8,128)}, bf16[2,32,24,192]{3,2,1,0:T(8,128)(2,1)S(1)}, bf16[2,32,24,2048]{3,1,2,0:T(8,128)(2,1)}, s32[]{:T(128)}, /*index=5*/s32[]{:T(128)}) while((s32[]{:T(128)}, f32[32,192,2048]{2,1,0:T(8,128)}, bf16[2,32,24,192]{3,2,1,0:T(8,128)(2,1)S(1)}, ...), condition=%wide.region_6.7_spmd.clone, body=%wide.region_5.6_spmd.clone.sunk | while | flops 654311424 | bytes 160825440 | solution.py:81
  278.2 4.0 constant_dynamic-slice_fusion.2
  282.2 13.8 %convolution_convert_fusion.3 = bf16[32,192,2048]{2,1,0:T(8,128)(2,1)} fusion(bf16[1,32,24,2048]{3,1,2,0:T(8,128)(2,1)} %constant_dynamic-slice_fusion.2, bf16[2,32,24,192]{3,2,1,0:T(8,128)(2,1)S(1)} %get-tuple-element.184, s32[]{:T(128)} %get-tuple-element.176), kind=kOutput, calls=%fused_computation.1.clone.1 | convolution fusion | flops 616562688 | bytes 28704772 | tf_op jit(solution)/shard_map/while/body/eval_jaxpr/jsf,jsd->jfd/dot_general | solution.py:77
  296.0 24.2 %select_add_fusion.2 = f32[32,192,2048]{2,1,0:T(8,128)} fusion(f32[32,192,2048]{2,1,0:T(8,128)} %get-tuple-element.177, bf16[32,192,2048]{2,1,0:T(8,128)(2,1)} %convolution_convert_fusion.3, pred[]{:T(512)S(6)} %compare.3), kind=kLoop, calls=%fused_computation.clone.1 | loop fusion | flops 37748736 | bytes 125829120 | tf_op jit(solution)/shard_map/while/body/eval_jaxpr/add | solution.py:79
  320.2 4.0 constant_dynamic-slice_fusion.2
  324.2 13.8 %convolution_convert_fusion.3 = bf16[32,192,2048]{2,1,0:T(8,128)(2,1)} fusion(bf16[1,32,24,2048]{3,1,2,0:T(8,128)(2,1)} %constant_dynamic-slice_fusion.2, bf16[2,32,24,192]{3,2,1,0:T(8,128)(2,1)S(1)} %get-tuple-element.184, s32[]{:T(128)} %get-tuple-element.176), kind=kOutput, calls=%fused_computation.1.clone.1 | convolution fusion | flops 616562688 | bytes 28704772 | tf_op jit(solution)/shard_map/while/body/eval_jaxpr/jsf,jsd->jfd/dot_general | solution.py:77
  338.0 40.1 %select_add_fusion.2 = f32[32,192,2048]{2,1,0:T(8,128)} fusion(f32[32,192,2048]{2,1,0:T(8,128)} %get-tuple-element.177, bf16[32,192,2048]{2,1,0:T(8,128)(2,1)} %convolution_convert_fusion.3, pred[]{:T(512)S(6)} %compare.3), kind=kLoop, calls=%fused_computation.clone.1 | loop fusion | flops 37748736 | bytes 125829120 | tf_op jit(solution)/shard_map/while/body/eval_jaxpr/add | solution.py:79
  378.1 26.0 %convert_element_type.132 = bf16[32,192,2048]{2,1,0:T(8,128)(2,1)} convert(f32[32,192,2048]{2,1,0:T(8,128)} %get-tuple-element.83) | non-fusion elementwise | flops 12582912 | bytes 75497472 | tf_op jit(solution)/shard_map/convert_element_type | solution.py:81
  (45 shorter events, 3.4 us)
Async XLA Ops:
  7.2 3.2 copy-start
  7.2 97.3 %all-gather.2.cloned.1.call-start = ((), (), s32[]{:S(2)}) async-start(), calls=%async_computation.4 | async-start | bytes 7864320 | tf_op jit(solution)/shard_map/all_gather | solution.py:43
  12.1 92.3 %copy-start.2 = (bf16[1,32,24,192]{3,2,1,0:T(8,128)(2,1)S(1)}, bf16[1,32,24,192]{3,2,1,0:T(8,128)(2,1)}, u32[]{:S(2)}) copy-start(bf16[1,32,24,192]{3,2,1,0:T(8,128)(2,1)} %param.12) | copy-start | bytes 884740
  12.1 92.3 %copy-start.3 = (bf16[1,32,24,192]{3,2,1,0:T(8,128)(2,1)S(1)}, bf16[1,32,24,192]{3,2,1,0:T(8,128)(2,1)}, u32[]{:S(2)}) copy-start(bf16[1,32,24,192]{3,2,1,0:T(8,128)(2,1)} %param.11) | copy-start | bytes 884740
  104.5 37.0 %copy-start.4 = (bf16[64,8]{0,1:T(8,128)(2,1)S(1)}, bf16[64,8]{0,1:T(8,128)(2,1)}, u32[]{:S(2)}) copy-start(bf16[64,8]{0,1:T(8,128)(2,1)} %param.10) | copy-start | bytes 3076
  136.8 10.3 %all-to-all-start.3 = ((f32[4,1,192]{2,1,0:T(1,128)}), f32[4,1,192]{2,1,0:T(1,128)S(1)}, u32[]{:S(2)}, u32[]{:S(2)}) async-start(f32[4,1,192]{2,1,0:T(1,128)} %reshape.97), calls=%async_computation.3 | async-start | bytes 8192 | tf_op jit(solution)/shard_map/all_to_all | solution.py:86
  150.0 29.6 %all-to-all-start = ((bf16[4,32,6]{1,2,0:T(8,128)(2,1)}), bf16[4,32,6]{1,2,0:T(8,128)(2,1)S(1)}, u32[]{:S(2)}, u32[]{:S(2)}) async-start(bf16[4,32,6]{1,2,0:T(8,128)(2,1)} %copy.64), calls=%async_computation | async-start | bytes 16384 | tf_op jit(solution)/shard_map/all_to_all | solution.py:41
  193.2 84.9 %all-to-all-start.2 = ((bf16[2,32,24,2048]{3,1,2,0:T(8,128)(2,1)}), bf16[2,32,24,2048]{3,1,2,0:T(8,128)(2,1)}, u32[]{:S(2)}, u32[]{:S(2)}) async-start(bf16[2,32,24,2048]{3,1,2,0:T(8,128)(2,1)} %copy.70), calls=%async_computation.2 | async-start | bytes 12582912 | tf_op jit(solution)/shard_map/all_to_all | solution.py:70
  378.1 26.0 %copy-start.1 = (bf16[64,4096]{1,0:T(8,128)(2,1)S(1)}, bf16[64,4096]{1,0:T(8,128)(2,1)}, u32[]{:S(2)}) copy-start(bf16[64,4096]{1,0:T(8,128)(2,1)} %param.8) | copy-start | bytes 1572868
Sparse Core Ops, SparseCore 0:
  58.9 45.5 all-gather.1
where the time goes:
time: 412 us; the launch traced here: 411 us
  blocking collectives  130 us (32%)
  other arithmetic  112 us (27%)
  waiting for transfers between devices  51.1 us (12%)
  matrix products  50.6 us (12%)
  local copies, waits for them, and re-layouts  38.7 us (9%)
  starting transfers between devices  14.5 us (4%)
  between operations  14.2 us (3%)
    all_gather x1, blocking collectives, on_device(): hidden_block = lax.all_gather(hidden[None], 'dp', axis=0, tiled=True)  76.2 us
    add x2, other arithmetic, add_member(): return summed + rounded.astype(jnp.float32)  64.3 us
    all_gather x1, waiting for transfers between devices, on_device(): gathered = lax.all_gather(arrived_rows, 'tensor', axis=3, tiled=True)  45.7 us
    all_to_all x1, blocking collectives, on_device(): lax.all_to_all(send_rows, 'expert', split_axis=0, concat_axis=0, tiled=True)  43.2 us
    dot_general x2, matrix products, add_member(): jnp.einsum('jsf,jsd->jfd', hid_one, col_one, preferred_element_type=jnp.f...  27.6 us
    convert_element_type x1, other arithmetic, on_device(): lax.fori_loop(0, hidden_block.shape[0], add_member, initial)  26 us
    dot_general x1, matrix products, on_device(): jnp.einsum('jsd,jfd->jsf', slot_rows, w_down, preferred_element_type=jnp....  21.3 us
    convert_element_type x1, local copies, waits for them, and re-layouts, on_device(): slot_rows.astype(jnp.float32)  16.9 us
  transfers between devices with their start and end apart: 4, of which 2 were waited for; matrix products, arithmetic and copies ran while one was open for 7% of the time, Pallas kernels for 0%

commit v1 on v0

--- a/solution.py
+++ b/solution.py
@@ -1,10 +1,13 @@
+import functools
 import jax
 import jax.numpy as jnp
 from jax import lax
+from jax.experimental import pallas as pl
+from jax.experimental.pallas import tpu as pltpu
 from jax.sharding import PartitionSpec as P
 
 
-def on_device(grad_out, route_ids, route_probs, gate_act, up_act, w_down):
+def on_device_wide(grad_out, route_ids, route_probs, gate_act, up_act, w_down):
     tok_count = grad_out.shape[0]
     top_count = route_ids.shape[1]
     expert_count = lax.axis_size("expert")
@@ -91,7 +94,228 @@
     return (grad_gate[None], grad_up[None], grad_weight, grad_probs)
 
 
+MESH = pl.DeviceIdType.MESH
+
+
+def collect_kernel(sizes, x_ref, meta_ref, hid_ref, tok, oth, metas, hid_oth, local, zs, zr, ms, mr, hs, hr, xs, xr, ys, yr, vs, vr, cs, cr):
+    tn, en, rn = sizes
+    t, e, d = lax.axis_index("tensor"), lax.axis_index("expert"), lax.axis_index("dp")
+    across = lax.rem(t + 2, tn)
+    mate = t + 1 - 2 * lax.rem(t, 2)
+    far = 1 - d
+    barrier = pltpu.get_barrier_semaphore()
+    others = []
+    for i in range(en):
+        for j in range(rn):
+            if i or j:
+                others.append((t, lax.rem(e + i, en), lax.rem(d + j, rn)))
+    peers = others + [(across, e, d), (mate, e, d)]
+    for peer in peers:
+        pl.semaphore_signal(barrier, inc=1, device_id=peer, device_id_type=MESH)
+    pl.semaphore_wait(barrier, len(peers))
+
+    def send(src, dst, ssem, rsem, peer):
+        copy = pltpu.make_async_remote_copy(
+            src_ref=src, dst_ref=dst, send_sem=ssem, recv_sem=rsem, device_id=peer, device_id_type=MESH
+        )
+        copy.start()
+        return copy
+
+    mine = [
+        pltpu.make_async_copy(x_ref, tok.at[t, e], local.at[0]),
+        pltpu.make_async_copy(meta_ref, metas.at[e, d], local.at[1]),
+    ]
+    for copy in mine:
+        copy.start()
+    z = [
+        send(x_ref, tok.at[t, e], zs.at[j - 1], zr.at[j - 1], (t, lax.rem(e + j, en), d))
+        for j in range(1, en)
+    ]
+    m = [send(meta_ref, metas.at[e, d], ms.at[i], mr.at[i], peer) for i, peer in enumerate(others)]
+    y = [send(x_ref, tok.at[t, e], ys.at[0], yr.at[0], (across, e, d))]
+    x = [send(x_ref.at[far], oth.at[t, e], xs.at[0], xr.at[0], (t, e, far))]
+    for j in range(1, en):
+        z[j - 1].wait_recv()
+        b = lax.rem(e - j + en, en)
+        x.append(send(tok.at[t, b, far], oth.at[t, b], xs.at[j], xr.at[j], (t, e, far)))
+        y.append(send(tok.at[t, b], tok.at[t, b], ys.at[j], yr.at[j], (across, e, d)))
+    h = send(hid_ref, hid_oth, hs, hr, (t, e, far))
+    v = []
+    for j in range(en):
+        x[j].wait_recv()
+        b = lax.rem(e - j + en, en)
+        v.append(send(oth.at[t, b], oth.at[t, b], vs.at[j], vr.at[j], (across, e, d)))
+    for copy in mine:
+        copy.wait()
+    c = [
+        send(tok.at[t], tok.at[t], cs.at[0], cr.at[0], (mate, e, d)),
+        send(oth.at[t], oth.at[t], cs.at[1], cr.at[1], (mate, e, d)),
+    ]
+    for copy in y:
+        copy.wait_recv()
+    c.append(send(tok.at[across], tok.at[across], cs.at[2], cr.at[2], (mate, e, d)))
+    for copy in v:
+        copy.wait_recv()
+    c.append(send(oth.at[across], oth.at[across], cs.at[3], cr.at[3], (mate, e, d)))
+    for copy in m + c + [h]:
+        copy.wait_recv()
+    for copy in z + m + y + x + v + c + [h]:
+        copy.wait_send()
+
+
+def return_kernel(sizes, x_ref, out, local, ss, rs):
+    tn, en = sizes
+    t, e, d = lax.axis_index("tensor"), lax.axis_index("expert"), lax.axis_index("dp")
+    barrier = pltpu.get_barrier_semaphore()
+    peers = []
+    for i in range(tn):
+        for j in range(en):
+            if i or j:
+                peers.append((lax.rem(t + i, tn), lax.rem(e + j, en), d))
+    for peer in peers:
+        pl.semaphore_signal(barrier, inc=1, device_id=peer, device_id_type=MESH)
+    pl.semaphore_wait(barrier, len(peers))
+    mine = pltpu.make_async_copy(x_ref.at[e], out.at[t, e], local)
+    mine.start()
+    copies = []
+    for i, peer in enumerate(peers):
+        copy = pltpu.make_async_remote_copy(
+            src_ref=x_ref.at[peer[1]], dst_ref=out.at[t, e], send_sem=ss.at[i], recv_sem=rs.at[i],
+            device_id=peer, device_id_type=MESH,
+        )
+        copy.start()
+        copies.append(copy)
+    mine.wait()
+    for copy in copies:
+        copy.wait()
+
+
+def expert_kernel(rows, scaled, hid_own, hid_far, gate, up, prob, w, grad_gate, grad_up, grad_w, dot):
+    slots = rows.shape[1]
+    turned = lax.dot_general(
+        w[0], rows[0], (((1,), (1,)), ((), ())), preferred_element_type=jnp.float32
+    )
+    grad_hidden = turned.T
+    g = gate[0, 0].astype(jnp.float32)
+    u = up[0, 0].astype(jnp.float32)
+    s = jax.nn.sigmoid(g)
+    silu = g * s
+    hidden = hid_own[0]
+    dot[0] = jnp.sum(grad_hidden * hidden.astype(jnp.float32), axis=1, keepdims=True)
+    weighted = prob[0] * grad_hidden
+    grad_up[0, 0] = (weighted * silu).astype(jnp.bfloat16)
+    grad_gate[0, 0] = (weighted * u * s * (1.0 + g * (1.0 - s))).astype(jnp.bfloat16)
+    both = jnp.concatenate([hidden.astype(jnp.float32), hid_far[0].astype(jnp.float32)], axis=0)
+    both = both.T.astype(jnp.bfloat16)
+    grad_w[0] = jnp.dot(both, scaled[0], preferred_element_type=jnp.float32).astype(jnp.bfloat16)
+
+
+def on_device(grad_out, route_ids, route_probs, gate_act, up_act, w_down):
+    tokens, width = grad_out.shape
+    top = route_ids.shape[1]
+    tn, en, rn = lax.axis_size("tensor"), lax.axis_size("expert"), lax.axis_size("dp")
+    t, e, d = lax.axis_index("tensor"), lax.axis_index("expert"), lax.axis_index("dp")
+    local, units, slots = w_down.shape[0], w_down.shape[1], gate_act.shape[2]
+    cap = slots // en
+    strip = width // (tn * rn)
+    half = width // rn
+    f32, bf16 = jnp.float32, jnp.bfloat16
+    sem = pltpu.SemaphoreType.DMA
+    vmem = pl.BlockSpec(memory_space=pltpu.VMEM)
+    g = gate_act[0].astype(f32)
+    hidden = (g * jax.nn.sigmoid(g) * up_act[0].astype(f32)).astype(bf16)
+    parts = jnp.transpose(grad_out.reshape(tokens, rn, tn, strip), (2, 1, 0, 3))
+    mine = lax.dynamic_index_in_dim(parts, t, 0, keepdims=False)
+    meta = jnp.concatenate([route_ids.T.astype(f32), route_probs.T.astype(f32)], axis=1)
+    tok, oth, metas, hid_far = pl.pallas_call(
+        functools.partial(collect_kernel, (tn, en, rn)),
+        out_shape=(
+            jax.ShapeDtypeStruct((tn, en, rn, tokens, strip), bf16),
+            jax.ShapeDtypeStruct((tn, en, tokens, strip), bf16),
+            jax.ShapeDtypeStruct((en, rn) + meta.shape, f32),
+            jax.ShapeDtypeStruct(hidden.shape, bf16),
+        ),
+        in_specs=[vmem] * 3,
+        out_specs=(vmem,) * 4,
+        scratch_shapes=[
+            sem((2,)), sem((en - 1,)), sem((en - 1,)), sem((en * rn - 1,)), sem((en * rn - 1,)), sem, sem,
+            sem((en,)), sem((en,)), sem((en,)), sem((en,)), sem((en,)), sem((en,)), sem((4,)), sem((4,)),
+        ],
+        compiler_params=pltpu.CompilerParams(collective_id=0, has_side_effects=True),
+    )(mine, meta, hidden)
+
+    ids = metas[..., :tokens].astype(jnp.int32)
+    probs = metas[..., tokens:]
+    here = e * local + jnp.arange(local, dtype=jnp.int32)
+    hit = ids[:, :, :, None, :] == here[:, None]
+    named = jnp.any(hit, axis=2)
+    weight = jnp.sum(jnp.where(hit, probs[:, :, :, None, :], 0.0), axis=2)
+    below = jnp.arange(tokens)[:, None] < jnp.arange(tokens)[None, :]
+    position = jnp.einsum("erxn,nm->erxm", named.astype(bf16), below.astype(bf16), preferred_element_type=f32)
+    place = jnp.where(named, position, -1.0)
+    spots = place[:, :, :, None, :] == jnp.arange(cap, dtype=f32)[:, None]
+    spots = jnp.transpose(spots, (1, 2, 0, 3, 4))
+    carried = jnp.transpose(weight, (1, 2, 0, 3))[:, :, :, None, :]
+    same = (jnp.arange(en)[:, None] == jnp.arange(en)[None, :])[None, None, :, None, :, None]
+    one = (spots[:, :, :, :, None, :] & same).reshape(rn, local * slots, en * tokens)
+    wide = jnp.where(spots, carried, 0.0)
+    slot_probs = lax.dynamic_index_in_dim(jnp.sum(wide, axis=-1), d, 0, keepdims=False).reshape(local, slots, 1)
+    wide = jnp.where(same, wide[:, :, :, :, None, :], 0.0).astype(bf16).reshape(rn, local * slots, en * tokens)
+    pick = lambda a, i: lax.dynamic_index_in_dim(a, i, 0, keepdims=False)
+    flat = jnp.transpose(tok, (1, 3, 2, 0, 4)).reshape(en * tokens, width)
+    far_flat = jnp.transpose(oth, (1, 2, 0, 3)).reshape(en * tokens, half)
+    near_flat = lax.dynamic_slice_in_dim(flat, d * half, half, 1)
+    rows = jnp.dot(pick(one, d).astype(bf16), flat, preferred_element_type=f32).astype(bf16).reshape(local, slots, width)
+    near = jnp.dot(pick(wide, d), near_flat, preferred_element_type=f32).astype(bf16).reshape(local, slots, half)
+    far = jnp.dot(pick(wide, 1 - d), far_flat, preferred_element_type=f32).astype(bf16).reshape(local, slots, half)
+    scaled = jnp.concatenate([near, far], axis=1)
+
+    def block(*shape):
+        return pl.BlockSpec((1,) + shape, lambda i: (i,) + (0,) * len(shape))
+
+    act = pl.BlockSpec((1, 1, slots, units), lambda i: (0, i, 0, 0))
+    act_shape = jax.ShapeDtypeStruct((1, local, slots, units), bf16)
+    grad_gate, grad_up, grad_w, dot = pl.pallas_call(
+        expert_kernel,
+        grid=(local,),
+        in_specs=[
+            block(slots, width), block(2 * slots, half), block(slots, units), block(slots, units), act, act,
+            block(slots, 1), block(units, width),
+        ],
+        out_specs=(act, act, block(units, half), block(slots, 1)),
+        out_shape=(
+            act_shape, act_shape,
+            jax.ShapeDtypeStruct((local, units, half), bf16),
+            jax.ShapeDtypeStruct((local, slots, 1), f32),
+        ),
+    )(rows, scaled, hidden, hid_far, gate_act, up_act, slot_probs, w_down)
+
+    cells = jnp.transpose(dot.reshape(local, en, cap), (1, 0, 2)).reshape(en, local * cap)
+    room = -(-local * cap // 1024) * 1024
+    cells = jnp.pad(cells, ((0, 0), (0, room - local * cap))).reshape(en, room // 128, 128)
+    back = pl.pallas_call(
+        functools.partial(return_kernel, (tn, en)),
+        out_shape=jax.ShapeDtypeStruct((tn,) + cells.shape, f32),
+        in_specs=[vmem],
+        out_specs=vmem,
+        scratch_shapes=[sem, sem((tn * en - 1,)), sem((tn * en - 1,))],
+        compiler_params=pltpu.CompilerParams(collective_id=1, has_side_effects=True),
+    )(cells)
+    back = jnp.sum(back, axis=0).reshape(en, room)[:, : local * cap].reshape(1, 1, -1)
+    every = jnp.arange(en * local, dtype=jnp.int32)
+    match = route_ids[:, :, None] == every
+    count = jnp.any(match, axis=1)
+    before = jnp.einsum("nx,nm->mx", count.astype(bf16), below.astype(bf16), preferred_element_type=f32)
+    at = jnp.sum(jnp.where(match, before[:, None, :], 0.0), axis=2).astype(jnp.int32)
+    target = route_ids * cap + at
+    chosen = target[:, :, None] == jnp.arange(en * local * cap, dtype=jnp.int32)
+    grad_probs = jnp.sum(jnp.where(chosen, back, 0.0), axis=2)
+    return grad_gate, grad_up, grad_w, grad_probs
+
+
 def solution(mesh):
+    sizes = mesh.shape
+    small = sizes["tensor"] == 4 and sizes["dp"] == 2 and sizes["expert"] <= 8
     placed = (
         P(("expert", "dp"), None),
         P(("expert", "dp"), None),
@@ -101,7 +325,7 @@
         P("expert", "tensor", None),
     )
     return jax.shard_map(
-        on_device,
+        on_device if small else on_device_wide,
         mesh=mesh,
         in_specs=placed,
         out_specs=(

time: 412 us -> 139 us (0.34)
  blocking collectives: 130 us -> 0 us
  other arithmetic: 112 us -> 12.3 us
  Pallas kernels: 0 us -> 94.9 us
  waiting for transfers between devices: 51.1 us -> 0 us
  matrix products: 50.6 us -> 9.07 us
  local copies, waits for them, and re-layouts: 38.7 us -> 21.2 us
  starting transfers between devices: 14.5 us -> 0 us
  between operations: 14.2 us -> 0.86 us
    pallas_call x0 -> x3, Pallas kernels: none -> 94.9 us  [the longest x1 51.3 us: on_device(): pl.pallas_call(expert_kernel, grid=(local,), in_specs=[block(slots, width...]
    all_gather x1 -> x0, blocking collectives: 76.2 us -> none  [on_device(): hidden_block = lax.all_gather(hidden[None], 'dp', axis=0, tiled=True)]
    add x4 -> x2, other arithmetic: 65 us -> 0.78 us  [the longest x1 0.78 us: on_device(): target = route_ids * cap + at]
    all_gather x1 -> x0, waiting for transfers between devices: 45.7 us -> none  [on_device(): gathered = lax.all_gather(arrived_rows, 'tensor', axis=3, tiled=True)]
    all_to_all x1 -> x0, blocking collectives: 43.2 us -> none  [on_device(): lax.all_to_all(send_rows, 'expert', split_axis=0, concat_axis=0, tiled=True)]
    dot_general x4 -> x5, matrix products: 50.6 us -> 9.07 us  [the longest x1 5.38 us: on_device(): jnp.dot(pick(one, d).astype(bf16), flat, preferred_element_type=f32)]
    convert_element_type x4 -> x3, other arithmetic: 35.6 us -> 3.89 us  [the longest x1 2.14 us: on_device(): hidden = (g * jax.nn.sigmoid(g) * up_act[0].astype(f32)).astype(bf16)]
    convert_element_type x7 -> x0, local copies, waits for them, and re-layouts: 18 us -> none  [the longest x1 16.9 us: on_device(): slot_rows.astype(jnp.float32)]
  transfers between devices with their start and end apart: 4 -> 0, of which waited for: 2 -> 0; matrix products, arithmetic and copies ran while one was open for 7% -> 0% of each run, Pallas kernels for 0% -> 0%
where the time goes in v1:
time: 139 us; the launch traced here: 138 us
  Pallas kernels  94.9 us (68%)
  local copies, waits for them, and re-layouts  21.2 us (15%)
  other arithmetic  12.3 us (9%)
  matrix products  9.07 us (7%)
    pallas_call x1, Pallas kernels, on_device(): pl.pallas_call(expert_kernel, grid=(local,), in_specs=[block(slots, width...  51.3 us
    pallas_call x1, Pallas kernels, on_device(): pl.pallas_call(functools.partial(collect_kernel, (tn, en, rn)), out_shape...  34 us
    pallas_call x1, Pallas kernels, on_device(): pl.pallas_call(functools.partial(return_kernel, (tn, en)), out_shape=jax....  9.61 us
    dot_general x1, matrix products, on_device(): jnp.dot(pick(one, d).astype(bf16), flat, preferred_element_type=f32)  5.38 us
    and x4, local copies, waits for them, and re-layouts, on_device(): spots[:, :, :, :, None, :] & same  3.68 us
    concatenate x1, other arithmetic, on_device(): scaled = jnp.concatenate([near, far], axis=1)  3.62 us
    unnamed x15, local copies, waits for them, and re-layouts  3.21 us
    transpose x1, local copies, waits for them, and re-layouts, on_device(): flat = jnp.transpose(tok, (1, 3, 2, 0, 4)).reshape(en * tokens, width)  3.21 us

profile of v1, /device:TPU:0, one launch (start us, length us, event | category | flops | bytes accessed | tf_op | source)
XLA Modules:
  0.0 138.3 jit_solution(426419056676716856)
XLA Ops:
  0.6 1.4 %reshape.87 = bf16[64,2,4,512]{3,2,1,0:T(4,128)(2,1)S(1)} reshape(bf16[64,4096]{1,0:T(8,128)(2,1)} %param.6) | data formatting | bytes 1048576 | tf_op jit(solution)/shard_map/reshape | solution.py:227
  2.1 0.3 constant_dynamic-slice_fusion.1
  2.4 0.7 copy.69
  3.1 0.8 copy.45
  4.5 0.8 convert_add_fusion
  5.3 0.7 convert_bitcast_fusion
  6.0 0.7 pad_maximum_fusion.1.meta_ref
  6.6 2.1 %fusion.7.hid_ref.hid_own = bf16[32,24,192]{2,1,0:T(8,128)(2,1)} fusion(bf16[1,32,24,192]{3,2,1,0:T(8,128)(2,1)} %up.1, bf16[1,32,24,192]{3,2,1,0:T(8,128)(2,1)} %gate.1), kind=kLoop, calls=%fused_computation.20 | loop fusion | flops 1179648 | bytes 884736 | tf_op jit(solution)/shard_map/convert_element_type | solution.py:226
  8.8 34.0 %shard_map.93 = (bf16[4,4,2,64,512]{4,3,2,1,0:T(8,128)(2,1)}, bf16[4,4,64,512]{3,2,1,0:T(8,128)(2,1)}, f32[4,2,8,128]{3,2,1,0:T(8,128)}, bf16[32,24,192]{2,1,0:T(8,128)(2,1)}) custom-call(bf16[2,64,512]{2,1,0:T(8,128)(2,1)} %bitcast.71, f32[8,128]{1,0:T(8,128)} %pad_maximum_fusion.1.meta_ref, bf16[32,24,192]{2,1,0:T(8,128)(2,1)} %fusion.7.hid_ref.hid_own), custom_call_target="tpu_custom_call" | custom-call | tf_op jit(solution)/shard_map/pallas_call | solution.py:230
  42.7 0.9 fusion.23
  44.7 0.5 broadcast_in_dim.95
  45.3 1.0 broadcast_in_dim.96
  46.5 0.6 and.32
  47.1 1.1 select_convert_fusion
  48.2 3.2 %copy.40 = bf16[4,64,2,4,512]{4,3,2,1,0:T(4,128)(2,1)S(1)} copy(bf16[4,64,2,4,512]{4,1,2,0,3:T(8,128)(2,1)} %bitcast.69) | data formatting | bytes 4194304 | tf_op jit(solution)/shard_map/transpose | solution.py:265
  51.4 2.8 %reshape.88 = bf16[256,4096]{1,0:T(8,128)(2,1)} reshape(bf16[4,64,2,4,512]{4,3,2,1,0:T(4,128)(2,1)S(1)} %copy.40) | data formatting | bytes 4194304 | tf_op jit(solution)/shard_map/reshape | solution.py:265
  54.2 2.3 %convolution_convert_fusion.2 = bf16[768,2048]{1,0:T(8,128)(2,1)S(1)} fusion(bf16[256,4096]{1,0:T(8,128)(2,1)} %reshape.88, s32[]{:T(128)S(6)} %select_n.58, bf16[2,768,256]{2,1,0:T(8,128)(2,1)} %select_convert_fusion, s32[]{:T(128)S(6)} %select_n.54), kind=kOutput, calls=%fused_computation.3 | convolution fusion | flops 806879232 | bytes 4587528 | tf_op jit(solution)/shard_map/dot_general | solution.py:269
  56.5 2.1 %copy.43 = bf16[4,64,4,512]{3,2,1,0:T(4,128)(2,1)S(1)} copy(bf16[4,64,4,512]{3,1,0,2:T(8,128)(2,1)} %bitcast.70) | data formatting | bytes 2097152 | tf_op jit(solution)/shard_map/transpose | solution.py:266
  58.9 1.0 convolution_convert_fusion.1
  59.9 3.6 %pad_maximum_fusion.scaled = bf16[32,48,2048]{2,1,0:T(8,128)(2,1)} fusion(bf16[32,24,2048]{2,1,0:T(8,128)(2,1)S(1)} %bitcast.65, bf16[32,24,2048]{2,1,0:T(8,128)(2,1)S(1)} %bitcast.66), kind=kLoop, calls=%fused_computation.1 | loop fusion | flops 12582912 | bytes 12582912 | tf_op jit(solution)/shard_map/concatenate | solution.py:271
  63.6 0.3 fusion.16
  63.9 1.0 copy.44.prob
  65.1 0.8 and.29
  65.9 2.1 %and.30 = pred[2,768,256]{2,1,0:T(32,128)(4,1)} reshape(pred[2,32,4,6,4,64]{5,4,3,2,1,0:T(4,128)(4,1)S(1)} %and.29) | data formatting | bytes 786432 | tf_op jit(solution)/shard_map/and | solution.py:260
  68.0 5.4 %convolution_convert_fusion = bf16[768,4096]{1,0:T(8,128)(2,1)} fusion(bf16[256,4096]{1,0:T(8,128)(2,1)S(1)} %copy-done, pred[2,768,256]{2,1,0:T(32,128)(4,1)} %and.30, s32[]{:T(128)S(6)} %select_n.54, pred[768,256]{1,0:T(8,128)(4,1)S(1)} %and.32), kind=kOutput, calls=%fused_computation | convolution fusion | flops 1613955072 | bytes 8781828 | tf_op jit(solution)/shard_map/dot_general | solution.py:268
  73.4 51.3 %shard_map.94 = (bf16[1,32,24,192]{3,2,1,0:T(8,128)(2,1)}, bf16[1,32,24,192]{3,2,1,0:T(8,128)(2,1)}, bf16[32,192,2048]{2,1,0:T(8,128)(2,1)}, f32[32,24,1]{2,1,0:T(8,128)}) custom-call(bf16[32,24,4096]{2,1,0:T(8,128)(2,1)} %bitcast.64, bf16[32,48,2048]{2,1,0:T(8,128)(2,1)} %pad_maximum_fusion.scaled, bf16[32,24,192]{2,1,0:T(8,128)(2,1)} %fusion.7.hid_ref.hid_own, ...), custom_call_target="tpu_custom_call" | custom-call | tf_op jit(solution)/shard_map/pallas_call | solution.py:278
  124.7 1.2 copy.48
  126.1 0.6 copy.71
  126.7 9.6 %shard_map.95 = f32[4,4,8,128]{3,2,1,0:T(8,128)} custom-call(f32[4,8,128]{2,1,0:T(8,128)} %bitcast.74), custom_call_target="tpu_custom_call" | custom-call | tf_op jit(solution)/shard_map/pallas_call | solution.py:296
  136.3 0.9 reduce_sum.48
  137.4 0.3 select_reduce_fusion
  137.7 0.7 copy.50
  (33 shorter events, 2.9 us)
Async XLA Ops:
  43.9 0.7 copy-start.2
  56.5 2.4 %copy-start.1 = (bf16[2,768,256]{2,1,0:T(8,128)(2,1)S(1)}, bf16[2,768,256]{2,1,0:T(8,128)(2,1)}, u32[]{:S(2)}) copy-start(bf16[2,768,256]{2,1,0:T(8,128)(2,1)} %select_convert_fusion) | copy-start | bytes 2359300
  59.9 3.6 %copy-start.3 = (f32[4,2,32,64]{3,2,1,0:T(8,128)S(1)}, f32[4,2,32,64]{3,2,1,0:T(8,128)}, u32[]{:S(2)}) copy-start(f32[4,2,32,64]{3,2,1,0:T(8,128)} %copy-done.2) | copy-start | bytes 196612
  63.6 4.4 %copy-start = (bf16[256,4096]{1,0:T(8,128)(2,1)S(1)}, bf16[256,4096]{1,0:T(8,128)(2,1)}, u32[]{:S(2)}) copy-start(bf16[256,4096]{1,0:T(8,128)(2,1)} %reshape.88) | copy-start | bytes 6291460
